TPU v7x, 32 devices: a whole 2x2x4 slice. The times are simulated.
32 devices in a mesh: rows: 8 (over z, x), cols: 4 (over y, core).
Axes of the slice: x: 2, y: 2, z: 4, core: 2. Of those that a mesh axis runs over, the one named last changes fastest.
Arguments:
- bag_index: int32 [512, 128], P(('rows', 'cols')), may hold values from 0 to 262143, as said below
- bag_length: int32 [512, 4], P(('rows', 'cols')), may hold values from 1 to 32
- emb_tables: float32 [4, 262144, 128], P(None, ('rows', 'cols')), may hold values from -0.6 to 0.6
- dense_feats: float32 [512, 128], P(('rows', 'cols')), may hold values from -6 to 6
- w_dense: float32 [128, 1024], replicated, may hold values from -0.5 to 0.5
- w_pair: float32 [10, 1024], replicated, may hold values from -0.5 to 0.5
- top_bias: float32 [1024], replicated, may hold values from -3 to 3
Outputs:
- pooled: float32 [512, 4, 128], P(('rows', 'cols'))
- top_hidden: float32 [512, 1024], P(('rows', 'cols'))
Inputs may be any that keep to these rules, and one draw needn't show every extreme that they name: `bag_length`: slots at or past a bag's length are ignored, whatever they hold. `bag_index`: device d holds rows d * 8192 to (d + 1) * 8192 - 1 of every table; among the 2048 slots (live or not) of the samples of one device, at most 128 hold rows of any one device, and in every draw some device's rows receive exactly 128 slots from every device.
All inputs are finite; a program needn't handle non-finite values.
Results may differ from a plain program's by a relative error of at most 0.0001.
Values sent between devices are 32-bit elements; how exact they have to be, the bound alone decides.
A program may use at most 128 MiB of HBM per device.

v0:
```python
import functools

import jax
import jax.numpy as jnp
from jax import lax
from jax.experimental import pallas as pl
from jax.experimental.pallas import tpu as pltpu
from jax.sharding import PartitionSpec as P

MESH = pl.DeviceIdType.MESH
F32 = jnp.float32
BF16 = jnp.bfloat16
LAG = 3
LAG_Z = 4
CHUNKS = 8


def kernel(
    dims,
    index_ref,
    length_ref,
    table_hbm,
    dense_ref,
    wd_hbm,
    wp_ref,
    bias_ref,
    pooled_ref,
    hidden_ref,
    table,
    wd,
    hidden,
    outbox,
    inbox,
    ids,
    rows_buf,
    core_out,
    core_in,
    keep,
    plane_out,
    plane_in,
    z_out,
    z_in,
    table_sem,
    wd_sem,
    box_send,
    box_recv,
    ids_sem,
    core_send,
    core_recv,
    plane_send,
    plane_recv,
    z_send,
    z_recv,
):
    nr, nc, nx, local_rows, nt, slots_bag, cap = dims
    n = nr * nc
    ny = nc // 2
    np_ = nx * ny
    nz = nr // nx
    groups = nz * np_
    samples, lanes = index_ref.shape
    width = table.shape[1]
    bags = samples * nt
    total_rows = nt * local_rows
    r = lax.axis_index("rows")
    c = lax.axis_index("cols")
    me = r * nc + c
    z, x, y, k = r // nx, r % nx, c // 2, c % 2
    p = x * ny + y

    def at(d):
        return {"rows": d // nc, "cols": d % nc}

    def place(zz, pp, kk):
        return zz * nx + pp // ny, (pp % ny) * 2 + kk

    def flat(zz, pp, kk):
        rr, cc = place(zz, pp, kk)
        return rr * nc + cc

    barrier = pltpu.get_barrier_semaphore()

    def greet(i, carry):
        d = (me + i) % n
        pl.semaphore_signal(barrier, inc=1, device_id=at(d), device_id_type=MESH)
        return carry

    lax.fori_loop(1, n, greet, 0)

    part = total_rows // CHUNKS
    table_copies = [
        pltpu.make_async_copy(
            table_hbm.at[pl.ds(i * part, part)], table.at[pl.ds(i * part, part)], table_sem.at[i]
        )
        for i in range(CHUNKS)
    ]
    wd_copy = pltpu.make_async_copy(wd_hbm, wd, wd_sem)
    for copy in table_copies:
        copy.start()
    wd_copy.start()

    idx = index_ref[...]
    lane = lax.broadcasted_iota(jnp.int32, (samples, lanes), 1)
    table_of = lane // slots_bag
    length = jnp.zeros((samples, lanes), jnp.int32)
    for t in range(nt):
        length = jnp.where(table_of == t, length_ref[:, t : t + 1], length)
    live = lane - table_of * slots_bag < length
    if local_rows & (local_rows - 1) == 0:
        owner = lax.shift_right_logical(idx, jnp.full_like(idx, local_rows.bit_length() - 1))
    else:
        owner = idx // local_rows
    row = table_of * local_rows + idx - owner * local_rows
    bag = table_of * samples + lax.broadcasted_iota(jnp.int32, (samples, lanes), 0)
    owner = jnp.where(live, owner, -1)
    pieces = []
    shift = 0
    while shift == 0 or (total_rows - 1) >> shift:
        pieces.append((row // (1 << shift)) % 256)
        shift += 8
    n_row = len(pieces)
    shift = 0
    while shift == 0 or bags >> shift:
        pieces.append(((bag + 1) // (1 << shift)) % 256)
        shift += 8
    pieces = [v.astype(F32) for v in pieces]
    dev_iota = lax.broadcasted_iota(jnp.int32, (n, lanes), 0)
    before = (
        lax.broadcasted_iota(jnp.int32, (lanes, lanes), 0)
        < lax.broadcasted_iota(jnp.int32, (lanes, lanes), 1)
    )
    before = jnp.where(before, 1.0, 0.0).astype(BF16)
    hots = [
        jnp.where(owner[b : b + 1, :] == dev_iota, 1.0, 0.0).astype(F32) for b in range(samples)
    ]
    prefix = jnp.dot(
        jnp.concatenate([h.astype(BF16) for h in hots], axis=0), before, preferred_element_type=F32
    )
    base = jnp.zeros((n, 1), F32)
    box = jnp.zeros((len(pieces) * n, cap), F32)
    cap_iota = lax.broadcasted_iota(jnp.int32, (cap, lanes), 0)
    for b in range(samples):
        hot = hots[b]
        rank = jnp.sum(hot * (prefix[b * n : (b + 1) * n, :] + base), axis=0, keepdims=True)
        base = base + jnp.sum(hot, axis=1, keepdims=True)
        spot = jnp.where(rank.astype(jnp.int32) == cap_iota, 1.0, 0.0).astype(BF16)
        coded = jnp.concatenate([hot * v[b : b + 1, :] for v in pieces], axis=0).astype(BF16)
        box = box + lax.dot_general(
            coded, spot, (((1,), (1,)), ((), ())), preferred_element_type=F32
        )
    box_row = jnp.zeros((n, cap), jnp.int32)
    box_bag = jnp.full((n, cap), -1, jnp.int32)
    for i in range(len(pieces)):
        piece = box[i * n : (i + 1) * n, :].astype(jnp.int32)
        if i < n_row:
            box_row = box_row + piece * (1 << (8 * i))
        else:
            box_bag = box_bag + piece * (1 << (8 * (i - n_row)))
    for d in range(n):
        outbox[d, 0:1, :] = box_row[d : d + 1, :]
        outbox[d, 1:2, :] = box_bag[d : d + 1, :]
    inbox[me] = outbox[me]

    pl.semaphore_wait(barrier, n - 1)

    def box_copy(d, source):
        return pltpu.make_async_remote_copy(
            src_ref=outbox.at[d],
            dst_ref=inbox.at[source],
            send_sem=box_send.at[d],
            recv_sem=box_recv.at[source],
            device_id=at(d),
            device_id_type=MESH,
        )

    def send_box(i, carry):
        box_copy((me + i) % n, me).start()
        return carry

    lax.fori_loop(1, n, send_box, 0)

    wd_copy.wait()
    hidden[...] = (
        jnp.dot(
            dense_ref[...], wd[...], precision=lax.Precision.HIGHEST, preferred_element_type=F32
        )
        + bias_ref[...]
    )

    def ids_copy(d):
        return pltpu.make_async_copy(inbox.at[d], ids.at[d], ids_sem.at[d])

    ids_copy(me).start()

    def take_box(i, carry):
        d = (me + n - i) % n
        box_copy((me + i) % n, d).wait_recv()
        ids_copy(d).start()
        return carry

    lax.fori_loop(1, n, take_box, 0)
    for d in range(n):
        ids_copy(d).wait()
    for copy in table_copies:
        copy.wait()

    bag_iota = lax.broadcasted_iota(jnp.int32, (bags, cap), 0)

    def inside(at_row):
        if total_rows & (total_rows - 1) == 0:
            return at_row & (total_rows - 1)
        return jnp.clip(at_row, 0, total_rows - 1)

    def fetch(d, slot):
        for i in range(cap):
            rows_buf[slot, i : i + 1, :] = table[pl.ds(inside(ids[d, 0, i]), 1), :]

    def pool(d, slot):
        found = rows_buf[slot]
        high = found.astype(BF16)
        low = (found - high.astype(F32)).astype(BF16)
        select = jnp.where(inbox[d, 1:2, :] == bag_iota, 1.0, 0.0).astype(BF16)
        both = jnp.dot(select, jnp.concatenate([high, low], axis=1), preferred_element_type=F32)
        return both[:, :width] + both[:, width:]

    def target(j):
        return (z + 1 + j // np_) % nz, (p + 1 + j % np_) % np_

    def core_copy(g):
        return pltpu.make_async_remote_copy(
            src_ref=core_out.at[g],
            dst_ref=core_in.at[g],
            send_sem=core_send.at[g],
            recv_sem=core_recv.at[g],
            device_id={"rows": r, "cols": y * 2 + 1 - k},
            device_id_type=MESH,
        )

    def plane_copy(zz, pp, source):
        rr, cc = place(z, pp, k)
        return pltpu.make_async_remote_copy(
            src_ref=plane_out.at[zz * np_ + pp],
            dst_ref=plane_in.at[zz * np_ + source],
            send_sem=plane_send.at[zz * np_ + pp],
            recv_sem=plane_recv.at[zz * np_ + source],
            device_id={"rows": rr, "cols": cc},
            device_id_type=MESH,
        )

    def z_copy(zz, source):
        rr, cc = place(zz, p, k)
        return pltpu.make_async_remote_copy(
            src_ref=z_out.at[zz],
            dst_ref=z_in.at[source],
            send_sem=z_send.at[zz],
            recv_sem=z_recv.at[source],
            device_id={"rows": rr, "cols": cc},
            device_id_type=MESH,
        )

    def step(it, carry):
        @pl.when(it < groups)
        def _():
            zz, pp = target(it)
            g = zz * np_ + pp
            mate = flat(zz, pp, 1 - k)
            own = flat(zz, pp, k)
            fetch(mate, 0)
            core_out[g] = pool(mate, 0)
            fetch(own, 1)
            keep[g] = pool(own, 1)
            core_copy(g).start()

        j = it - LAG

        @pl.when((j >= 0) & (j < groups))
        def _():
            zz, pp = target(j)
            g = zz * np_ + pp
            core_copy(g).wait_recv()
            summed = core_in[g] + keep[g]

            @pl.when(j % np_ == np_ - 1)
            def _():
                plane_in[g] = summed

            @pl.when(j % np_ < np_ - 1)
            def _():
                plane_out[g] = summed
                plane_copy(zz, pp, p).start()

        h = it - LAG - LAG_Z

        @pl.when((h >= 0) & (h % np_ == np_ - 1))
        def _():
            zi = h // np_
            zz = (z + 1 + zi) % nz
            summed = plane_in[zz * np_ + p]
            for i in range(1, np_):
                other = (p + i) % np_
                plane_copy(zz, other, other).wait_recv()
                summed = summed + plane_in[zz * np_ + other]

            @pl.when(zi < nz - 1)
            def _():
                z_out[zz] = summed
                z_copy(zz, z).start()

            @pl.when(zi == nz - 1)
            def _():
                z_in[z] = summed

        return carry

    lax.fori_loop(0, groups + LAG + LAG_Z, step, 0)

    pooled = z_in[z]
    for i in range(1, nz):
        other = (z + i) % nz
        z_copy(other, other).wait_recv()
        pooled = pooled + z_in[other]

    feats = [dense_ref[...]]
    for t in range(nt):
        feats.append(pooled[t * samples : (t + 1) * samples, :])
        pooled_ref[:, t, :] = feats[-1]
    total = hidden[...]
    pair = 0
    for first in range(nt + 1):
        for second in range(first + 1, nt + 1):
            dots = jnp.sum(feats[first] * feats[second], axis=-1, keepdims=True)
            total = total + dots * wp_ref[pair : pair + 1, :]
            pair += 1
    hidden_ref[...] = jnp.maximum(total, 0.0)

    def drain_box(i, carry):
        box_copy((me + i) % n, me).wait_send()
        return carry

    lax.fori_loop(1, n, drain_box, 0)

    def drain(j, carry):
        zz, pp = target(j)
        core_copy(zz * np_ + pp).wait_send()

        @pl.when(j % np_ < np_ - 1)
        def _():
            plane_copy(zz, pp, p).wait_send()

        return carry

    lax.fori_loop(0, groups, drain, 0)
    for i in range(1, nz):
        z_copy((z + i) % nz, z).wait_send()


def shards(nr, nc, bag_index, bag_length, emb_tables, dense_feats, w_dense, w_pair, top_bias):
    samples, lanes = bag_index.shape
    nt, local_rows, width = emb_tables.shape
    n = nr * nc
    slots = samples * lanes
    cap = 2 * slots // n
    bags = samples * nt
    units = w_dense.shape[1]
    nx = 2 if nr % 2 == 0 else 1
    groups = n // 2
    nz = nr // nx
    dims = (nr, nc, nx, local_rows, nt, lanes // nt, cap)
    vmem = pl.BlockSpec(memory_space=pltpu.VMEM)
    anyw = pl.BlockSpec(memory_space=pl.ANY)
    blocks = lambda m: pltpu.VMEM((m, bags, width), F32)
    dma = pltpu.SemaphoreType.DMA
    pooled, hidden = pl.pallas_call(
        functools.partial(kernel, dims),
        out_shape=(
            jax.ShapeDtypeStruct((samples, nt, width), F32),
            jax.ShapeDtypeStruct((samples, units), F32),
        ),
        in_specs=[vmem, vmem, anyw, vmem, anyw, vmem, vmem],
        out_specs=(vmem, vmem),
        scratch_shapes=[
            pltpu.VMEM((nt * local_rows, width), F32),
            pltpu.VMEM(w_dense.shape, F32),
            pltpu.VMEM((samples, units), F32),
            pltpu.VMEM((n, 2, cap), jnp.int32),
            pltpu.VMEM((n, 2, cap), jnp.int32),
            pltpu.SMEM((n, 2, cap), jnp.int32),
            pltpu.VMEM((2, cap, width), F32),
            blocks(groups),
            blocks(groups),
            blocks(groups),
            blocks(groups),
            blocks(groups),
            blocks(nz),
            blocks(nz),
            dma((CHUNKS,)),
            dma,
            dma((n,)),
            dma((n,)),
            dma((n,)),
            dma((groups,)),
            dma((groups,)),
            dma((groups,)),
            dma((groups,)),
            dma((nz,)),
            dma((nz,)),
        ],
        compiler_params=pltpu.CompilerParams(
            collective_id=0, has_side_effects=True, vmem_limit_bytes=60 * 1024 * 1024
        ),
    )(
        bag_index,
        bag_length,
        emb_tables.reshape(nt * local_rows, width),
        dense_feats,
        w_dense,
        w_pair,
        top_bias.reshape(1, units),
    )
    return pooled, hidden


def solution(mesh):
    nr, nc = mesh.shape["rows"], mesh.shape["cols"]
    in_specs = (
        P(("rows", "cols"), None),
        P(("rows", "cols"), None),
        P(None, ("rows", "cols"), None),
        P(("rows", "cols"), None),
        P(),
        P(),
        P(),
    )
    out_specs = (P(("rows", "cols"), None, None), P(("rows", "cols"), None))
    return jax.shard_map(
        functools.partial(shards, nr, nc),
        mesh=mesh,
        in_specs=in_specs,
        out_specs=out_specs,
        check_vma=False,
    )
```

profile of v0, /device:TPU:0, one launch (start us, length us, event | category | flops | bytes accessed | tf_op | source)
XLA Modules:
  0.0 33.7 jit_solution(13626603231987745030)
XLA Ops:
  0.6 1.4 %copy.9.length_ref = s32[16,4]{1,0:T(8,128)} copy(s32[16,4]{0,1:T(4,128)} %param.8) | data formatting | bytes 512 | tf_op args[1]
  2.0 28.9 %shard_map.86 = (f32[16,4,128]{2,1,0:T(4,128)}, f32[16,1024]{1,0:T(8,128)}) custom-call(s32[16,128]{1,0:T(8,128)} %index_ref.1, s32[16,4]{1,0:T(8,128)} %copy.9.length_ref, f32[32768,128]{1,0:T(8,128)} %bitcast.2, f32[16,128]{1,0:T(8,128)} %dense_ref.1, f32[128,1024]{1,0:T(8,128)} %wd_hbm.1, f32[10,1024]{1,0:T(8,128)} %wp_ref.1, f32[1,1024]{1,0:T(1,128)} %bitcast.3), custom_call_target="tpu_custom_call" | custom-call | tf_op jit(solution)/shard_map/pallas_call | solution.py:373
  30.9 1.4 %copy.12 = f32[16,4,128]{2,1,0:T(4,128)} copy(f32[16,4,128]{2,1,0:T(4,128)} %get-tuple-element.4) | data formatting | bytes 65536
  32.3 1.5 %copy.13 = f32[16,1024]{1,0:T(8,128)} copy(f32[16,1024]{1,0:T(8,128)} %get-tuple-element.5) | data formatting | bytes 131072
where the time goes:
time: 34 us; the launch traced here: 33.7 us
  Pallas kernels  28.9 us (85%)
  local copies, waits for them, and re-layouts  4.2 us (12%)
  between operations  0.64 us (2%)
    pallas_call x1, Pallas kernels, shards(): pl.pallas_call(functools.partial(kernel, dims), out_shape=(jax.ShapeDtype...  28.9 us
    unnamed x3, local copies, waits for them, and re-layouts  4.2 us

commit v1 on v0

v1 whole, which is shorter than its diff:
```python
import functools

import jax
import jax.numpy as jnp
from jax import lax
from jax.experimental import pallas as pl
from jax.experimental.pallas import tpu as pltpu
from jax.sharding import PartitionSpec as P

LOGICAL = pl.DeviceIdType.LOGICAL
F32 = jnp.float32
BF16 = jnp.bfloat16
LAG = 5
CHUNKS = 8


def kernel(
    dims,
    index_hbm,
    length_hbm,
    table_hbm,
    dense_hbm,
    wd_hbm,
    wp_hbm,
    bias_hbm,
    pooled_ref,
    hidden_ref,
    index_ref,
    length_ref,
    table,
    dense_ref,
    wd,
    wp_ref,
    bias_ref,
    row_out,
    bag_out,
    bag_in,
    ids,
    rows_a,
    rows_b,
    rows_c,
    rows_d,
    core_out,
    core_in,
    keep,
    plane_out,
    plane_in,
    z_out,
    z_in,
    load_sem,
    table_sem,
    box_send,
    box_recv,
    core_send,
    core_recv,
    plane_send,
    plane_recv,
    z_send,
    z_recv,
):
    nr, nc, nx, local_rows, nt, slots_bag, cap = dims
    n = nr * nc
    ny = nc // 2
    np_ = nx * ny
    nz = nr // nx
    groups = nz * np_
    samples, lanes = index_ref.shape
    width = table.shape[1]
    bags = samples * nt
    total_rows = nt * local_rows
    r = lax.axis_index("rows")
    c = lax.axis_index("cols")
    z, x, y, k = r // nx, r % nx, c // 2, c % 2

    hops = sorted(
        [(dx, dy) for dx in range(nx) for dy in range(ny)],
        key=lambda h: (-min(h[0], nx - h[0]) - min(h[1], ny - h[1]), h),
    )
    back = [hops.index(((-dx) % nx, (-dy) % ny)) for dx, dy in hops]

    def plane_at(i):
        if i == nz - 1:
            return z
        low = jnp.where(nz - 1 - i > z, nz - 1 - i, nz - 2 - i)
        high = jnp.where(i < z, i, i + 1)
        return jnp.where(2 * z < nz, low, high)

    def turn_at(zz):
        low = jnp.where(z > zz, nz - 1 - z, nz - 2 - z)
        high = jnp.where(z < zz, z, z - 1)
        return jnp.where(2 * zz < nz, low, high)

    planes = [plane_at(i) for i in range(nz)]
    turns = [turn_at(planes[i]) for i in range(nz - 1)] + [nz - 1]
    chips = [(((x + dx) % nx), ((y + dy) % ny)) for dx, dy in hops]

    def flat(zz, chip, kk):
        return (zz * nx + chip[0]) * nc + chip[1] * 2 + kk

    peers = []
    for i in range(nz):
        for q in range(np_):
            for same in range(2):
                if (i, q, same) != (nz - 1, np_ - 1, 1):
                    d = flat(planes[i], chips[q], k if same else 1 - k)
                    peers.append((d, (turns[i] * np_ + back[q]) * 2 + same))
    own_slot = n - 1

    load = lambda i, source, target: pltpu.make_async_copy(source, target, load_sem.at[i])
    index_copy = load(0, index_hbm, index_ref)
    length_copy = load(1, length_hbm, length_ref)
    wd_copy = load(2, wd_hbm, wd)
    dense_copy = load(3, dense_hbm, dense_ref)
    wp_copy = load(4, wp_hbm, wp_ref)
    bias_copy = load(5, bias_hbm, bias_ref)
    index_copy.start()
    length_copy.start()
    barrier = pltpu.get_barrier_semaphore()
    for d, slot in peers:
        pl.semaphore_signal(barrier, inc=1, device_id=d, device_id_type=LOGICAL)
    wd_copy.start()
    dense_copy.start()
    bias_copy.start()
    wp_copy.start()
    part = total_rows // CHUNKS
    for i in range(CHUNKS):
        rows = pl.ds(i * part, part)
        pltpu.make_async_copy(table_hbm.at[rows], table.at[rows], table_sem).start()

    index_copy.wait()
    length_copy.wait()
    idx = index_ref[...]
    lane = lax.broadcasted_iota(jnp.int32, (samples, lanes), 1)
    table_of = lane // slots_bag
    length = length_ref[...].astype(F32)
    diagonal = (
        lax.broadcasted_iota(jnp.int32, (samples, samples), 0)
        == lax.broadcasted_iota(jnp.int32, (samples, samples), 1)
    )
    lengths = jnp.zeros((samples, lanes), F32)
    for t in range(nt):
        column = jnp.sum(jnp.where(diagonal, length[t : t + 1, :], 0.0), axis=1, keepdims=True)
        lengths = jnp.where(table_of == t, column, lengths)
    live = lane - table_of * slots_bag < lengths.astype(jnp.int32)
    if local_rows & (local_rows - 1) == 0:
        owner = lax.shift_right_logical(idx, jnp.full_like(idx, local_rows.bit_length() - 1))
    else:
        owner = idx // local_rows
    row = table_of * local_rows + idx - owner * local_rows
    bag = lax.broadcasted_iota(jnp.int32, (samples, lanes), 0) * nt + table_of
    owner = jnp.where(live, owner, -1)
    pieces = []
    shift = 0
    while shift == 0 or (total_rows - 1) >> shift:
        pieces.append((row // (1 << shift)) % 256)
        shift += 8
    n_row = len(pieces)
    shift = 0
    while shift == 0 or bags >> shift:
        pieces.append(((bag + 1) // (1 << shift)) % 256)
        shift += 8
    pieces = [v.astype(F32) for v in pieces]
    dev_iota = lax.broadcasted_iota(jnp.int32, (n, lanes), 0)
    before = (
        lax.broadcasted_iota(jnp.int32, (lanes, lanes), 0)
        < lax.broadcasted_iota(jnp.int32, (lanes, lanes), 1)
    )
    before = jnp.where(before, 1.0, 0.0).astype(BF16)
    hots = [
        jnp.where(owner[b : b + 1, :] == dev_iota, 1.0, 0.0).astype(F32) for b in range(samples)
    ]
    prefix = jnp.dot(
        jnp.concatenate([h.astype(BF16) for h in hots], axis=0), before, preferred_element_type=F32
    )
    base = jnp.zeros((n, 1), F32)
    box = jnp.zeros((len(pieces) * n, cap), F32)
    cap_iota = lax.broadcasted_iota(jnp.int32, (cap, lanes), 0)
    for b in range(samples):
        hot = hots[b]
        rank = jnp.sum(hot * (prefix[b * n : (b + 1) * n, :] + base), axis=0, keepdims=True)
        base = base + jnp.sum(hot, axis=1, keepdims=True)
        spot = jnp.where(rank.astype(jnp.int32) == cap_iota, 1.0, 0.0).astype(BF16)
        coded = jnp.concatenate([hot * v[b : b + 1, :] for v in pieces], axis=0).astype(BF16)
        box = box + lax.dot_general(
            coded, spot, (((1,), (1,)), ((), ())), preferred_element_type=F32
        )
    box_row = jnp.zeros((n, cap), jnp.int32)
    box_bag = jnp.full((n, cap), -1, jnp.int32)
    for i in range(len(pieces)):
        piece = box[i * n : (i + 1) * n, :].astype(jnp.int32)
        if i < n_row:
            box_row = box_row + piece * (1 << (8 * i))
        else:
            box_bag = box_bag + piece * (1 << (8 * (i - n_row)))
    if total_rows & (total_rows - 1) == 0:
        box_row = box_row & (total_rows - 1)
    else:
        box_row = jnp.clip(box_row, 0, total_rows - 1)
    for d in range(n):
        row_out[d] = box_row[d : d + 1, :]
        bag_out[d] = box_bag[d : d + 1, :]

    pl.semaphore_wait(barrier, n - 1)

    def box_copy(source, target, which, d, slot):
        return pltpu.make_async_remote_copy(
            src_ref=source.at[d],
            dst_ref=target.at[slot],
            send_sem=box_send.at[which],
            recv_sem=box_recv.at[which],
            device_id=d,
            device_id_type=LOGICAL,
        )

    for d, slot in peers:
        box_copy(row_out, ids, 0, d, slot).start()
    for d, slot in peers:
        box_copy(bag_out, bag_in, 1, d, slot).start()
    me = r * nc + c
    own_ids = load(0, row_out.at[me], ids.at[own_slot])
    own_ids.start()
    bag_in[own_slot] = bag_out[me]

    wd_copy.wait()
    dense_copy.wait()
    bias_copy.wait()
    wp_copy.wait()
    dense = dense_ref[...]
    hidden_ref[...] = (
        jnp.dot(dense, wd[...], precision=lax.Precision.HIGHEST, preferred_element_type=F32)
        + bias_ref[...]
    )

    own_ids.wait()
    pltpu.make_async_copy(table_hbm, table, table_sem).wait()
    others = pl.ds(0, n - 1)
    for which, (source, target) in enumerate(((row_out, ids), (bag_out, bag_in))):
        pltpu.make_async_remote_copy(
            src_ref=source.at[others],
            dst_ref=target.at[others],
            send_sem=box_send.at[which],
            recv_sem=box_recv.at[which],
            device_id=me,
            device_id_type=LOGICAL,
        ).wait_recv()

    bag_iota = lax.broadcasted_iota(jnp.int32, (bags, cap), 0)
    buffers = ((rows_a, rows_b), (rows_c, rows_d))

    def fetch(slot, target):
        for i in range(cap):
            target[i : i + 1, :] = table[pl.ds(ids[slot, 0, i], 1), :]

    def pool(slot, source):
        found = source[...]
        high = found.astype(BF16)
        low = (found - high.astype(F32)).astype(BF16)
        select = jnp.where(bag_in[slot] == bag_iota, 1.0, 0.0).astype(BF16)
        both = jnp.dot(select, jnp.concatenate([high, low], axis=1), preferred_element_type=F32)
        return both[:, :width] + both[:, width:]

    def copy(source, target, send, recv, d):
        return pltpu.make_async_remote_copy(
            src_ref=source,
            dst_ref=target,
            send_sem=send,
            recv_sem=recv,
            device_id=d,
            device_id_type=LOGICAL,
        )

    mate = flat(z, (x, y), 1 - k)

    def core_copy(j):
        return copy(core_out.at[j], core_in.at[j], core_send, core_recv.at[j], mate)

    def forward(j):
        i, q = j // np_, j % np_
        core_copy(j).wait_recv()
        summed = core_in[j] + keep[j]
        if q == np_ - 1:
            keep[j] = summed
        else:
            at = i * (np_ - 1) + q
            to = i * (np_ - 1) + back[q]
            plane_out[at] = summed
            copy(
                plane_out.at[at],
                plane_in.at[to],
                plane_send,
                plane_recv.at[i],
                flat(z, chips[q], k),
            ).start()

    def collect(i):
        some = pl.ds(i * (np_ - 1), np_ - 1)
        copy(plane_out.at[some], plane_in.at[some], plane_send, plane_recv.at[i], me).wait_recv()
        summed = keep[i * np_ + np_ - 1]
        for q in range(np_ - 1):
            summed = summed + plane_in[i * (np_ - 1) + q]
        if i < nz - 1:
            z_out[i] = summed
            copy(
                z_out.at[i], z_in.at[turns[i]], z_send, z_recv, flat(planes[i], (x, y), k)
            ).start()
        return summed

    for j in range(groups + 1):
        if j < groups:
            fetch(2 * j, buffers[j % 2][0])
            fetch(2 * j + 1, buffers[j % 2][1])
        if j > 0:
            core_out[j - 1] = pool(2 * j - 2, buffers[(j - 1) % 2][0])
            keep[j - 1] = pool(2 * j - 1, buffers[(j - 1) % 2][1])
            core_copy(j - 1).start()
        if j >= LAG:
            forward(j - LAG)
    for j in range(groups + 1 - LAG, groups):
        forward(j)
    for i in range(nz):
        pooled = collect(i)
    if nz > 1:
        copy(z_out, z_in, z_send, z_recv, me).wait_recv()
        for i in range(nz - 1):
            pooled = pooled + z_in[i]

    pooled_ref[...] = pooled
    feats = [dense] + [pooled_ref[pl.ds(t, samples, stride=nt), :] for t in range(nt)]
    total = hidden_ref[...]
    pair = 0
    for first in range(nt + 1):
        for second in range(first + 1, nt + 1):
            dots = jnp.sum(feats[first] * feats[second], axis=-1, keepdims=True)
            total = total + dots * wp_ref[pair : pair + 1, :]
            pair += 1
    hidden_ref[...] = total

    for which, (source, target) in enumerate(((row_out, ids), (bag_out, bag_in))):
        pltpu.make_async_remote_copy(
            src_ref=source.at[others],
            dst_ref=target.at[others],
            send_sem=box_send.at[which],
            recv_sem=box_recv.at[which],
            device_id=me,
            device_id_type=LOGICAL,
        ).wait_send()
    copy(core_out, core_in, core_send, core_recv.at[0], me).wait_send()
    if np_ > 1:
        copy(plane_out, plane_in, plane_send, plane_recv.at[0], me).wait_send()
    if nz > 1:
        copy(z_out, z_in, z_send, z_recv, me).wait_send()


def finish(pooled_ref, total_ref, pooled_out, hidden_out):
    pooled_out[...] = pooled_ref[...]
    hidden_out[...] = jnp.maximum(total_ref[...], 0.0)


def shards(nr, nc, bag_index, bag_length, emb_tables, dense_feats, w_dense, w_pair, top_bias):
    samples, lanes = bag_index.shape
    nt, local_rows, width = emb_tables.shape
    n = nr * nc
    slots = samples * lanes
    cap = 2 * slots // n
    bags = samples * nt
    units = w_dense.shape[1]
    nx = 2 if nr % 2 == 0 else 1
    groups = n // 2
    nz = nr // nx
    np_ = groups // nz
    dims = (nr, nc, nx, local_rows, nt, lanes // nt, cap)
    vmem = pl.BlockSpec(memory_space=pltpu.VMEM)
    hbm = pl.BlockSpec(memory_space=pltpu.HBM)
    blocks = lambda m: pltpu.VMEM((max(m, 1), bags, width), F32)
    dma = pltpu.SemaphoreType.DMA
    results = (
        jax.ShapeDtypeStruct((bags, width), F32),
        jax.ShapeDtypeStruct((samples, units), F32),
    )
    total_rows = nt * local_rows
    pooled, total = pl.pallas_call(
        functools.partial(kernel, dims),
        out_shape=(pltpu.VMEM((bags, width), F32), pltpu.VMEM((samples, units), F32)),
        in_specs=[hbm] * 7,
        out_specs=(vmem, vmem),
        scratch_shapes=[
            pltpu.VMEM((samples, lanes), jnp.int32),
            pltpu.VMEM((nt, samples), jnp.int32),
            pltpu.VMEM((total_rows, width), F32),
            pltpu.VMEM((samples, width), F32),
            pltpu.VMEM(w_dense.shape, F32),
            pltpu.VMEM(w_pair.shape, F32),
            pltpu.VMEM((1, units), F32),
            pltpu.VMEM((n, 1, cap), jnp.int32),
            pltpu.VMEM((n, 1, cap), jnp.int32),
            pltpu.VMEM((n, 1, cap), jnp.int32),
            pltpu.SMEM((n, 1, cap), jnp.int32),
            pltpu.VMEM((cap, width), F32),
            pltpu.VMEM((cap, width), F32),
            pltpu.VMEM((cap, width), F32),
            pltpu.VMEM((cap, width), F32),
            blocks(groups),
            blocks(groups),
            blocks(groups),
            blocks(nz * (np_ - 1)),
            blocks(nz * (np_ - 1)),
            blocks(nz - 1),
            blocks(nz - 1),
            dma((6,)),
            dma,
            dma((2,)),
            dma((2,)),
            dma,
            dma((groups,)),
            dma,
            dma((nz,)),
            dma,
            dma,
        ],
        compiler_params=pltpu.CompilerParams(
            collective_id=0, has_side_effects=True, vmem_limit_bytes=64000 * 1024
        ),
    )(
        bag_index,
        bag_length.T,
        emb_tables.reshape(total_rows, width),
        dense_feats,
        w_dense,
        w_pair,
        top_bias.reshape(1, units),
    )
    pooled, hidden = pl.pallas_call(
        finish,
        out_shape=results,
        in_specs=[vmem, vmem],
        out_specs=(vmem, vmem),
        compiler_params=pltpu.CompilerParams(vmem_limit_bytes=4 * 1024 * 1024),
    )(pooled, total)
    return pooled.reshape(samples, nt, width), hidden


def solution(mesh):
    nr, nc = mesh.shape["rows"], mesh.shape["cols"]
    in_specs = (
        P(("rows", "cols"), None),
        P(("rows", "cols"), None),
        P(None, ("rows", "cols"), None),
        P(("rows", "cols"), None),
        P(),
        P(),
        P(),
    )
    out_specs = (P(("rows", "cols"), None, None), P(("rows", "cols"), None))
    return jax.shard_map(
        functools.partial(shards, nr, nc),
        mesh=mesh,
        in_specs=in_specs,
        out_specs=out_specs,
        check_vma=False,
    )
```

time: 34 us -> 23.3 us (0.69)
  Pallas kernels: 28.9 us -> 22.4 us
  local copies, waits for them, and re-layouts: 4.2 us -> 0 us
    pallas_call x1 -> x2, Pallas kernels: 28.9 us -> 22.4 us  [the longest x1 21.8 us: shards(): pl.pallas_call(functools.partial(kernel, dims), out_shape=(pltpu.VMEM((ba...]
    unnamed x3 -> x0, local copies, waits for them, and re-layouts: 4.2 us -> none
where the time goes in v1:
time: 23.3 us; the launch traced here: 23.1 us
  Pallas kernels  22.4 us (96%)
  between operations  0.64 us (3%)
    pallas_call x1, Pallas kernels, shards(): pl.pallas_call(functools.partial(kernel, dims), out_shape=(pltpu.VMEM((ba...  21.8 us
    pallas_call x1, Pallas kernels, shards(): pl.pallas_call(finish, out_shape=results, in_specs=[vmem, vmem], out_spec...  0.65 us

profile of v1, /device:TPU:0, one launch (start us, length us, event | category | flops | bytes accessed | tf_op | source)
XLA Modules:
  0.0 23.1 jit_solution(5236054012345769714)
XLA Ops:
  0.6 21.8 %shard_map.86 = (f32[64,128]{1,0:T(8,128)S(1)}, f32[16,1024]{1,0:T(8,128)S(1)}) custom-call(s32[16,128]{1,0:T(8,128)} %index_hbm.1, s32[4,16]{1,0:T(4,128)} %bitcast.6, f32[32768,128]{1,0:T(8,128)} %bitcast.4, f32[16,128]{1,0:T(8,128)} %dense_hbm.1, f32[128,1024]{1,0:T(8,128)} %wd_hbm.1, f32[10,1024]{1,0:T(8,128)} %wp_hbm.1, f32[1,1024]{1,0:T(1,128)} %bitcast.5), custom_call_target="tpu_custom_call" | custom-call | tf_op jit(solution)/shard_map/pallas_call | solution.py:381
  22.4 0.6 %shard_map.87 = (f32[64,128]{1,0:T(8,128)}, f32[16,1024]{1,0:T(8,128)}) custom-call(f32[64,128]{1,0:T(8,128)S(1)} %get-tuple-element.6.pooled_ref, f32[16,1024]{1,0:T(8,128)S(1)} %get-tuple-element.7.total_ref), custom_call_target="tpu_custom_call" | custom-call | tf_op jit(solution)/shard_map/pallas_call | solution.py:432

commit v2 on v1

--- a/solution.py
+++ b/solution.py
@@ -11,7 +11,16 @@
 F32 = jnp.float32
 BF16 = jnp.bfloat16
 LAG = 5
+DIRECT = 1
 CHUNKS = 8
+
+
+def near_pairs(nz):
+    last = {}
+    for z in range(nz):
+        turns = [zz for zz in (range(nz - 1, -1, -1) if 2 * z < nz else range(nz)) if zz != z]
+        last[z] = turns[-1] if turns else z
+    return nz > 1 and all(last[last[z]] == z for z in range(nz))
 
 
 def kernel(
@@ -47,6 +56,8 @@
     plane_in,
     z_out,
     z_in,
+    near_out,
+    near_in,
     load_sem,
     table_sem,
     box_send,
@@ -57,11 +68,14 @@
     plane_recv,
     z_send,
     z_recv,
+    near_send,
+    near_recv,
 ):
     nr, nc, nx, local_rows, nt, slots_bag, cap = dims
     n = nr * nc
     ny = nc // 2
     np_ = nx * ny
+    around = 2 * np_
     nz = nr // nx
     groups = nz * np_
     samples, lanes = index_ref.shape
@@ -97,15 +111,17 @@
     def flat(zz, chip, kk):
         return (zz * nx + chip[0]) * nc + chip[1] * 2 + kk
 
+    me = flat(z, (x, y), k)
+    mate = flat(z, (x, y), 1 - k)
     peers = []
     for i in range(nz):
         for q in range(np_):
             for same in range(2):
                 if (i, q, same) != (nz - 1, np_ - 1, 1):
                     d = flat(planes[i], chips[q], k if same else 1 - k)
-                    peers.append((d, (turns[i] * np_ + back[q]) * 2 + same))
-    own_slot = n - 1
-
+                    peers.append((d, turns[i], back[q] * 2 + same))
+
+    near = near_pairs(nz)
     load = lambda i, source, target: pltpu.make_async_copy(source, target, load_sem.at[i])
     index_copy = load(0, index_hbm, index_ref)
     length_copy = load(1, length_hbm, length_ref)
@@ -116,16 +132,16 @@
     index_copy.start()
     length_copy.start()
     barrier = pltpu.get_barrier_semaphore()
-    for d, slot in peers:
+    for d, turn, slot in peers:
         pl.semaphore_signal(barrier, inc=1, device_id=d, device_id_type=LOGICAL)
+    part = total_rows // CHUNKS
+    for i in range(CHUNKS):
+        rows = pl.ds(i * part, part)
+        pltpu.make_async_copy(table_hbm.at[rows], table.at[rows], table_sem).start()
     wd_copy.start()
     dense_copy.start()
     bias_copy.start()
     wp_copy.start()
-    part = total_rows // CHUNKS
-    for i in range(CHUNKS):
-        rows = pl.ds(i * part, part)
-        pltpu.make_async_copy(table_hbm.at[rows], table.at[rows], table_sem).start()
 
     index_copy.wait()
     length_copy.wait()
@@ -200,65 +216,6 @@
         row_out[d] = box_row[d : d + 1, :]
         bag_out[d] = box_bag[d : d + 1, :]
 
-    pl.semaphore_wait(barrier, n - 1)
-
-    def box_copy(source, target, which, d, slot):
-        return pltpu.make_async_remote_copy(
-            src_ref=source.at[d],
-            dst_ref=target.at[slot],
-            send_sem=box_send.at[which],
-            recv_sem=box_recv.at[which],
-            device_id=d,
-            device_id_type=LOGICAL,
-        )
-
-    for d, slot in peers:
-        box_copy(row_out, ids, 0, d, slot).start()
-    for d, slot in peers:
-        box_copy(bag_out, bag_in, 1, d, slot).start()
-    me = r * nc + c
-    own_ids = load(0, row_out.at[me], ids.at[own_slot])
-    own_ids.start()
-    bag_in[own_slot] = bag_out[me]
-
-    wd_copy.wait()
-    dense_copy.wait()
-    bias_copy.wait()
-    wp_copy.wait()
-    dense = dense_ref[...]
-    hidden_ref[...] = (
-        jnp.dot(dense, wd[...], precision=lax.Precision.HIGHEST, preferred_element_type=F32)
-        + bias_ref[...]
-    )
-
-    own_ids.wait()
-    pltpu.make_async_copy(table_hbm, table, table_sem).wait()
-    others = pl.ds(0, n - 1)
-    for which, (source, target) in enumerate(((row_out, ids), (bag_out, bag_in))):
-        pltpu.make_async_remote_copy(
-            src_ref=source.at[others],
-            dst_ref=target.at[others],
-            send_sem=box_send.at[which],
-            recv_sem=box_recv.at[which],
-            device_id=me,
-            device_id_type=LOGICAL,
-        ).wait_recv()
-
-    bag_iota = lax.broadcasted_iota(jnp.int32, (bags, cap), 0)
-    buffers = ((rows_a, rows_b), (rows_c, rows_d))
-
-    def fetch(slot, target):
-        for i in range(cap):
-            target[i : i + 1, :] = table[pl.ds(ids[slot, 0, i], 1), :]
-
-    def pool(slot, source):
-        found = source[...]
-        high = found.astype(BF16)
-        low = (found - high.astype(F32)).astype(BF16)
-        select = jnp.where(bag_in[slot] == bag_iota, 1.0, 0.0).astype(BF16)
-        both = jnp.dot(select, jnp.concatenate([high, low], axis=1), preferred_element_type=F32)
-        return both[:, :width] + both[:, width:]
-
     def copy(source, target, send, recv, d):
         return pltpu.make_async_remote_copy(
             src_ref=source,
@@ -269,7 +226,40 @@
             device_id_type=LOGICAL,
         )
 
-    mate = flat(z, (x, y), 1 - k)
+    pl.semaphore_wait(barrier, n - 1)
+    boxes = ((row_out, ids), (bag_out, bag_in))
+    for i, (source, target) in enumerate(boxes):
+        for d, turn, slot in peers:
+            copy(
+                source.at[d], target.at[turn, slot], box_send.at[i], box_recv.at[i, turn], d
+            ).start()
+    own_ids = load(0, row_out.at[me], ids.at[nz - 1, around - 1])
+    own_ids.start()
+    bag_in[nz - 1, around - 1] = bag_out[me]
+
+    own_ids.wait()
+    pltpu.make_async_copy(table_hbm, table, table_sem).wait()
+    def boxes_from(i):
+        some = pl.ds(0, around - 1 if i == nz - 1 else around)
+        for which, (source, target) in enumerate(boxes):
+            copy(
+                source.at[some], target.at[i, some], box_send.at[which], box_recv.at[which, i], me
+            ).wait_recv()
+
+    bag_iota = lax.broadcasted_iota(jnp.int32, (bags, cap), 0)
+    buffers = ((rows_a, rows_b), (rows_c, rows_d))
+
+    def fetch(i, slot, target):
+        for at in range(cap):
+            target[at : at + 1, :] = table[pl.ds(ids[i, slot, 0, at], 1), :]
+
+    def pool(i, slot, source):
+        found = source[...]
+        high = found.astype(BF16)
+        low = (found - high.astype(F32)).astype(BF16)
+        select = jnp.where(bag_in[i, slot] == bag_iota, 1.0, 0.0).astype(BF16)
+        both = jnp.dot(select, jnp.concatenate([high, low], axis=1), preferred_element_type=F32)
+        return both[:, :width] + both[:, width:]
 
     def core_copy(j):
         return copy(core_out.at[j], core_in.at[j], core_send, core_recv.at[j], mate)
@@ -278,11 +268,15 @@
         i, q = j // np_, j % np_
         core_copy(j).wait_recv()
         summed = core_in[j] + keep[j]
-        if q == np_ - 1:
+        if near and i == nz - 2 and q < DIRECT:
+            near_out[q] = summed
+            copy(
+                near_out.at[q], near_in.at[back[q]], near_send, near_recv, flat(planes[i], chips[q], k)
+            ).start()
+        elif q == np_ - 1:
             keep[j] = summed
         else:
-            at = i * (np_ - 1) + q
-            to = i * (np_ - 1) + back[q]
+            at, to = i * (np_ - 1) + q, i * (np_ - 1) + back[q]
             plane_out[at] = summed
             copy(
                 plane_out.at[at],
@@ -293,10 +287,12 @@
             ).start()
 
     def collect(i):
-        some = pl.ds(i * (np_ - 1), np_ - 1)
+        skip = DIRECT if near and i == nz - 2 else 0
+        first = i * (np_ - 1) + skip
+        some = pl.ds(first, np_ - 1 - skip)
         copy(plane_out.at[some], plane_in.at[some], plane_send, plane_recv.at[i], me).wait_recv()
         summed = keep[i * np_ + np_ - 1]
-        for q in range(np_ - 1):
+        for q in range(skip, np_ - 1):
             summed = summed + plane_in[i * (np_ - 1) + q]
         if i < nz - 1:
             z_out[i] = summed
@@ -305,20 +301,41 @@
             ).start()
         return summed
 
-    for j in range(groups + 1):
-        if j < groups:
-            fetch(2 * j, buffers[j % 2][0])
-            fetch(2 * j + 1, buffers[j % 2][1])
-        if j > 0:
-            core_out[j - 1] = pool(2 * j - 2, buffers[(j - 1) % 2][0])
-            keep[j - 1] = pool(2 * j - 1, buffers[(j - 1) % 2][1])
-            core_copy(j - 1).start()
-        if j >= LAG:
-            forward(j - LAG)
-    for j in range(groups + 1 - LAG, groups):
-        forward(j)
+    order = list(range(groups))
+    seen = set()
+    for step in range(groups + LAG):
+        if step < groups:
+            i, q = order[step] // np_, order[step] % np_
+            if i not in seen:
+                seen.add(i)
+                boxes_from(i)
+            fetch(i, 2 * q, buffers[step % 2][0])
+            fetch(i, 2 * q + 1, buffers[step % 2][1])
+        if 0 < step <= groups:
+            j = order[step - 1]
+            i, q = j // np_, j % np_
+            core_out[j] = pool(i, 2 * q, buffers[(step - 1) % 2][0])
+            keep[j] = pool(i, 2 * q + 1, buffers[(step - 1) % 2][1])
+            core_copy(j).start()
+        if step >= LAG:
+            forward(order[step - LAG])
+
     for i in range(nz):
+        if i == nz - 1:
+            wd_copy.wait()
+            dense_copy.wait()
+            bias_copy.wait()
+            wp_copy.wait()
+            dense = dense_ref[...]
+            hidden_ref[...] = (
+                jnp.dot(dense, wd[...], precision=lax.Precision.HIGHEST, preferred_element_type=F32)
+                + bias_ref[...]
+            )
         pooled = collect(i)
+    if near:
+        copy(near_out, near_in, near_send, near_recv, me).wait_recv()
+        for q in range(DIRECT):
+            pooled = pooled + near_in[q]
     if nz > 1:
         copy(z_out, z_in, z_send, z_recv, me).wait_recv()
         for i in range(nz - 1):
@@ -335,20 +352,20 @@
             pair += 1
     hidden_ref[...] = total
 
-    for which, (source, target) in enumerate(((row_out, ids), (bag_out, bag_in))):
-        pltpu.make_async_remote_copy(
-            src_ref=source.at[others],
-            dst_ref=target.at[others],
-            send_sem=box_send.at[which],
-            recv_sem=box_recv.at[which],
-            device_id=me,
-            device_id_type=LOGICAL,
+    others = pl.ds(0, n - 1)
+    for which, (source, target) in enumerate(boxes):
+        copy(
+            source.at[others], source.at[others], box_send.at[which], box_recv.at[which, 0], me
         ).wait_send()
     copy(core_out, core_in, core_send, core_recv.at[0], me).wait_send()
-    if np_ > 1:
-        copy(plane_out, plane_in, plane_send, plane_recv.at[0], me).wait_send()
+    whole = pl.ds(0, nz * (np_ - 1) - (DIRECT if near else 0))
+    copy(
+        plane_out.at[whole], plane_in.at[whole], plane_send, plane_recv.at[0], me
+    ).wait_send()
     if nz > 1:
         copy(z_out, z_in, z_send, z_recv, me).wait_send()
+    if near:
+        copy(near_out, near_in, near_send, near_recv, me).wait_send()
 
 
 def finish(pooled_ref, total_ref, pooled_out, hidden_out):
@@ -393,8 +410,8 @@
             pltpu.VMEM((1, units), F32),
             pltpu.VMEM((n, 1, cap), jnp.int32),
             pltpu.VMEM((n, 1, cap), jnp.int32),
-            pltpu.VMEM((n, 1, cap), jnp.int32),
-            pltpu.SMEM((n, 1, cap), jnp.int32),
+            pltpu.VMEM((nz, 2 * np_, 1, cap), jnp.int32),
+            pltpu.SMEM((nz, 2 * np_, 1, cap), jnp.int32),
             pltpu.VMEM((cap, width), F32),
             pltpu.VMEM((cap, width), F32),
             pltpu.VMEM((cap, width), F32),
@@ -406,14 +423,18 @@
             blocks(nz * (np_ - 1)),
             blocks(nz - 1),
             blocks(nz - 1),
+            blocks(DIRECT),
+            blocks(DIRECT),
             dma((6,)),
             dma,
             dma((2,)),
-            dma((2,)),
+            dma((2, nz)),
             dma,
             dma((groups,)),
             dma,
             dma((nz,)),
+            dma,
+            dma,
             dma,
             dma,
         ],

time: 23.3 us -> 22.8 us (0.979)
  Pallas kernels: 22.4 us -> 21.9 us
    pallas_call x1, Pallas kernels: 21.8 us -> 21.3 us  [shards(): pl.pallas_call(functools.partial(kernel, dims), out_shape=(pltpu.VMEM((ba...]
where the time goes in v2:
time: 22.8 us; the launch traced here: 22.5 us
  Pallas kernels  21.9 us (96%)
  between operations  0.64 us (3%)
    pallas_call x1, Pallas kernels, shards(): pl.pallas_call(functools.partial(kernel, dims), out_shape=(pltpu.VMEM((ba...  21.3 us
    pallas_call x1, Pallas kernels, shards(): pl.pallas_call(finish, out_shape=results, in_specs=[vmem, vmem], out_spec...  0.65 us

profile of v2, /device:TPU:0, one launch (start us, length us, event | category | flops | bytes accessed | tf_op | source)
XLA Modules:
  0.0 22.5 jit_solution(3845154411964970768)
XLA Ops:
  0.6 21.3 %shard_map.86 = (f32[64,128]{1,0:T(8,128)S(1)}, f32[16,1024]{1,0:T(8,128)S(1)}) custom-call(s32[16,128]{1,0:T(8,128)} %index_hbm.1, s32[4,16]{1,0:T(4,128)} %bitcast.6, f32[32768,128]{1,0:T(8,128)} %bitcast.4, f32[16,128]{1,0:T(8,128)} %dense_hbm.1, f32[128,1024]{1,0:T(8,128)} %wd_hbm.1, f32[10,1024]{1,0:T(8,128)} %wp_hbm.1, f32[1,1024]{1,0:T(1,128)} %bitcast.5), custom_call_target="tpu_custom_call" | custom-call | tf_op jit(solution)/shard_map/pallas_call | solution.py:398
  21.9 0.6 %shard_map.87 = (f32[64,128]{1,0:T(8,128)}, f32[16,1024]{1,0:T(8,128)}) custom-call(f32[64,128]{1,0:T(8,128)S(1)} %get-tuple-element.6.pooled_ref, f32[16,1024]{1,0:T(8,128)S(1)} %get-tuple-element.7.total_ref), custom_call_target="tpu_custom_call" | custom-call | tf_op jit(solution)/shard_map/pallas_call | solution.py:453

commit v3 on v2

--- a/solution.py
+++ b/solution.py
@@ -11,16 +11,7 @@
 F32 = jnp.float32
 BF16 = jnp.bfloat16
 LAG = 5
-DIRECT = 1
 CHUNKS = 8
-
-
-def near_pairs(nz):
-    last = {}
-    for z in range(nz):
-        turns = [zz for zz in (range(nz - 1, -1, -1) if 2 * z < nz else range(nz)) if zz != z]
-        last[z] = turns[-1] if turns else z
-    return nz > 1 and all(last[last[z]] == z for z in range(nz))
 
 
 def kernel(
@@ -56,8 +47,6 @@
     plane_in,
     z_out,
     z_in,
-    near_out,
-    near_in,
     load_sem,
     table_sem,
     box_send,
@@ -68,8 +57,6 @@
     plane_recv,
     z_send,
     z_recv,
-    near_send,
-    near_recv,
 ):
     nr, nc, nx, local_rows, nt, slots_bag, cap = dims
     n = nr * nc
@@ -93,16 +80,10 @@
     back = [hops.index(((-dx) % nx, (-dy) % ny)) for dx, dy in hops]
 
     def plane_at(i):
-        if i == nz - 1:
-            return z
-        low = jnp.where(nz - 1 - i > z, nz - 1 - i, nz - 2 - i)
-        high = jnp.where(i < z, i, i + 1)
-        return jnp.where(2 * z < nz, low, high)
+        return z if i == nz - 1 else jnp.where(i < z, i, i + 1)
 
     def turn_at(zz):
-        low = jnp.where(z > zz, nz - 1 - z, nz - 2 - z)
-        high = jnp.where(z < zz, z, z - 1)
-        return jnp.where(2 * zz < nz, low, high)
+        return jnp.where(z < zz, z, z - 1)
 
     planes = [plane_at(i) for i in range(nz)]
     turns = [turn_at(planes[i]) for i in range(nz - 1)] + [nz - 1]
@@ -115,13 +96,14 @@
     mate = flat(z, (x, y), 1 - k)
     peers = []
     for i in range(nz):
+        far = z if i == nz - 1 else jnp.where(2 * z < nz, planes[nz - 2 - i], planes[i])
+        turn = nz - 1 if i == nz - 1 else turn_at(far)
         for q in range(np_):
             for same in range(2):
                 if (i, q, same) != (nz - 1, np_ - 1, 1):
-                    d = flat(planes[i], chips[q], k if same else 1 - k)
-                    peers.append((d, turns[i], back[q] * 2 + same))
-
-    near = near_pairs(nz)
+                    d = flat(far, chips[q], k if same else 1 - k)
+                    peers.append((d, turn, back[q] * 2 + same))
+
     load = lambda i, source, target: pltpu.make_async_copy(source, target, load_sem.at[i])
     index_copy = load(0, index_hbm, index_ref)
     length_copy = load(1, length_hbm, length_ref)
@@ -268,12 +250,7 @@
         i, q = j // np_, j % np_
         core_copy(j).wait_recv()
         summed = core_in[j] + keep[j]
-        if near and i == nz - 2 and q < DIRECT:
-            near_out[q] = summed
-            copy(
-                near_out.at[q], near_in.at[back[q]], near_send, near_recv, flat(planes[i], chips[q], k)
-            ).start()
-        elif q == np_ - 1:
+        if q == np_ - 1:
             keep[j] = summed
         else:
             at, to = i * (np_ - 1) + q, i * (np_ - 1) + back[q]
@@ -287,12 +264,10 @@
             ).start()
 
     def collect(i):
-        skip = DIRECT if near and i == nz - 2 else 0
-        first = i * (np_ - 1) + skip
-        some = pl.ds(first, np_ - 1 - skip)
+        some = pl.ds(i * (np_ - 1), np_ - 1)
         copy(plane_out.at[some], plane_in.at[some], plane_send, plane_recv.at[i], me).wait_recv()
         summed = keep[i * np_ + np_ - 1]
-        for q in range(skip, np_ - 1):
+        for q in range(np_ - 1):
             summed = summed + plane_in[i * (np_ - 1) + q]
         if i < nz - 1:
             z_out[i] = summed
@@ -332,10 +307,6 @@
                 + bias_ref[...]
             )
         pooled = collect(i)
-    if near:
-        copy(near_out, near_in, near_send, near_recv, me).wait_recv()
-        for q in range(DIRECT):
-            pooled = pooled + near_in[q]
     if nz > 1:
         copy(z_out, z_in, z_send, z_recv, me).wait_recv()
         for i in range(nz - 1):
@@ -358,14 +329,9 @@
             source.at[others], source.at[others], box_send.at[which], box_recv.at[which, 0], me
         ).wait_send()
     copy(core_out, core_in, core_send, core_recv.at[0], me).wait_send()
-    whole = pl.ds(0, nz * (np_ - 1) - (DIRECT if near else 0))
-    copy(
-        plane_out.at[whole], plane_in.at[whole], plane_send, plane_recv.at[0], me
-    ).wait_send()
+    copy(plane_out, plane_in, plane_send, plane_recv.at[0], me).wait_send()
     if nz > 1:
         copy(z_out, z_in, z_send, z_recv, me).wait_send()
-    if near:
-        copy(near_out, near_in, near_send, near_recv, me).wait_send()
 
 
 def finish(pooled_ref, total_ref, pooled_out, hidden_out):
@@ -423,8 +389,6 @@
             blocks(nz * (np_ - 1)),
             blocks(nz - 1),
             blocks(nz - 1),
-            blocks(DIRECT),
-            blocks(DIRECT),
             dma((6,)),
             dma,
             dma((2,)),
@@ -433,8 +397,6 @@
             dma((groups,)),
             dma,
             dma((nz,)),
-            dma,
-            dma,
             dma,
             dma,
         ],

time: 22.8 us -> 22.3 us (0.978)
  Pallas kernels: 21.9 us -> 21.5 us
    pallas_call x1, Pallas kernels: 21.3 us -> 20.9 us  [shards(): pl.pallas_call(functools.partial(kernel, dims), out_shape=(pltpu.VMEM((ba...]
where the time goes in v3:
time: 22.3 us; the launch traced here: 22.1 us
  Pallas kernels  21.5 us (96%)
  between operations  0.64 us (3%)
    pallas_call x1, Pallas kernels, shards(): pl.pallas_call(functools.partial(kernel, dims), out_shape=(pltpu.VMEM((ba...  20.9 us
    pallas_call x1, Pallas kernels, shards(): pl.pallas_call(finish, out_shape=results, in_specs=[vmem, vmem], out_spec...  0.65 us

profile of v3, /device:TPU:0, one launch (start us, length us, event | category | flops | bytes accessed | tf_op | source)
XLA Modules:
  0.0 22.1 jit_solution(5890942336525605157)
XLA Ops:
  0.6 20.9 %shard_map.86 = (f32[64,128]{1,0:T(8,128)S(1)}, f32[16,1024]{1,0:T(8,128)S(1)}) custom-call(s32[16,128]{1,0:T(8,128)} %index_hbm.1, s32[4,16]{1,0:T(4,128)} %bitcast.6, f32[32768,128]{1,0:T(8,128)} %bitcast.4, f32[16,128]{1,0:T(8,128)} %dense_hbm.1, f32[128,1024]{1,0:T(8,128)} %wd_hbm.1, f32[10,1024]{1,0:T(8,128)} %wp_hbm.1, f32[1,1024]{1,0:T(1,128)} %bitcast.5), custom_call_target="tpu_custom_call" | custom-call | tf_op jit(solution)/shard_map/pallas_call | solution.py:364
  21.5 0.6 %shard_map.87 = (f32[64,128]{1,0:T(8,128)}, f32[16,1024]{1,0:T(8,128)}) custom-call(f32[64,128]{1,0:T(8,128)S(1)} %get-tuple-element.6.pooled_ref, f32[16,1024]{1,0:T(8,128)S(1)} %get-tuple-element.7.total_ref), custom_call_target="tpu_custom_call" | custom-call | tf_op jit(solution)/shard_map/pallas_call | solution.py:415

commit v4 on v3

--- a/solution.py
+++ b/solution.py
@@ -10,7 +10,7 @@
 LOGICAL = pl.DeviceIdType.LOGICAL
 F32 = jnp.float32
 BF16 = jnp.bfloat16
-LAG = 5
+LAG = 4
 CHUNKS = 8
 
 
@@ -307,6 +307,13 @@
                 + bias_ref[...]
             )
         pooled = collect(i)
+    others = pl.ds(0, n - 1)
+    for which, (source, target) in enumerate(boxes):
+        copy(
+            source.at[others], source.at[others], box_send.at[which], box_recv.at[which, 0], me
+        ).wait_send()
+    copy(core_out, core_in, core_send, core_recv.at[0], me).wait_send()
+    copy(plane_out, plane_in, plane_send, plane_recv.at[0], me).wait_send()
     if nz > 1:
         copy(z_out, z_in, z_send, z_recv, me).wait_recv()
         for i in range(nz - 1):
@@ -323,13 +330,6 @@
             pair += 1
     hidden_ref[...] = total
 
-    others = pl.ds(0, n - 1)
-    for which, (source, target) in enumerate(boxes):
-        copy(
-            source.at[others], source.at[others], box_send.at[which], box_recv.at[which, 0], me
-        ).wait_send()
-    copy(core_out, core_in, core_send, core_recv.at[0], me).wait_send()
-    copy(plane_out, plane_in, plane_send, plane_recv.at[0], me).wait_send()
     if nz > 1:
         copy(z_out, z_in, z_send, z_recv, me).wait_send()
 

time: 22.3 us -> 22.1 us (level)
  no operation moved by 1% of the time
where the time goes in v4:
time: 22.1 us; the launch traced here: 21.9 us
  Pallas kernels  21.3 us (96%)
  between operations  0.64 us (3%)
    pallas_call x1, Pallas kernels, shards(): pl.pallas_call(functools.partial(kernel, dims), out_shape=(pltpu.VMEM((ba...  20.6 us
    pallas_call x1, Pallas kernels, shards(): pl.pallas_call(finish, out_shape=results, in_specs=[vmem, vmem], out_spec...  0.65 us

profile of v4, /device:TPU:0, one launch (start us, length us, event | category | flops | bytes accessed | tf_op | source)
XLA Modules:
  0.0 21.9 jit_solution(5008306486033154719)
XLA Ops:
  0.6 20.6 %shard_map.86 = (f32[64,128]{1,0:T(8,128)S(1)}, f32[16,1024]{1,0:T(8,128)S(1)}) custom-call(s32[16,128]{1,0:T(8,128)} %index_hbm.1, s32[4,16]{1,0:T(4,128)} %bitcast.6, f32[32768,128]{1,0:T(8,128)} %bitcast.4, f32[16,128]{1,0:T(8,128)} %dense_hbm.1, f32[128,1024]{1,0:T(8,128)} %wd_hbm.1, f32[10,1024]{1,0:T(8,128)} %wp_hbm.1, f32[1,1024]{1,0:T(1,128)} %bitcast.5), custom_call_target="tpu_custom_call" | custom-call | tf_op jit(solution)/shard_map/pallas_call | solution.py:364
  21.3 0.6 %shard_map.87 = (f32[64,128]{1,0:T(8,128)}, f32[16,1024]{1,0:T(8,128)}) custom-call(f32[64,128]{1,0:T(8,128)S(1)} %get-tuple-element.6.pooled_ref, f32[16,1024]{1,0:T(8,128)S(1)} %get-tuple-element.7.total_ref), custom_call_target="tpu_custom_call" | custom-call | tf_op jit(solution)/shard_map/pallas_call | solution.py:415
